TPU v7x, 32 devices: a whole 2x2x4 slice. The times are simulated.
32 devices in a mesh: state: 2 (over x), bond: 16 (over z, y, core).
Axes of the slice: x: 2, y: 2, z: 4, core: 2. Of those that a mesh axis runs over, the one named last changes fastest.
Arguments:
- intersect_left: bfloat16 [2, 2048, 2048], P('state', 'bond'), may hold values from -0.125 to 0.125
- stored_block: bfloat16 [2, 4, 2048, 2048], P('state', None, 'bond'), may hold values from -6 to 6
- stored_site: bfloat16 [2, 2, 2048, 2048], P('state', None, 'bond'), may hold values from -6 to 6
- current_site: bfloat16 [2048, 2, 2048], P('bond', None, 'state'), may hold values from -0.09375 to 0.09375
- current_block: bfloat16 [4, 2048, 2048], P(None, 'bond', 'state'), may hold values from -6 to 6
- penalty_weight: float32 [2], replicated, may hold values from 0.5 to 4
Outputs:
- penalized: float32 [4, 2048, 2048], P(None, 'bond', 'state')
- intersect_next: bfloat16 [2, 2048, 2048], P('state', 'bond')
All inputs are finite; a program needn't handle non-finite values.
Results may differ from a plain program's by a relative error of at most 0.0055.
Values may be sent and summed in bfloat16 or wider, within the bound.
A program may use at most 64 MiB of HBM per device.

v0:
```python
import jax
import jax.numpy as jnp
from jax import lax
from jax.sharding import PartitionSpec as P


def contract_last(left, right):
    return lax.dot_general(
        left, right, (((1,), (1,)), ((), ())), preferred_element_type=jnp.float32
    )


def shards(intersect_left, stored_block, stored_site, current_site, current_block, penalty_weight):
    bond_width = intersect_left.shape[2]
    column_count = stored_block.shape[2]
    pair_count = stored_block.shape[1]
    physical = stored_site.shape[1]
    operand = jnp.concatenate(
        [
            stored_block[0].reshape(pair_count * column_count, bond_width),
            stored_site[0].reshape(physical * column_count, bond_width),
        ],
        axis=0,
    )
    products = contract_last(operand, lax.all_gather(intersect_left, "bond", axis=1, tiled=True)[0])
    projected = products[: pair_count * column_count].reshape(pair_count, column_count, bond_width)
    moved = (
        products[pair_count * column_count :]
        .astype(jnp.bfloat16)
        .reshape(1, physical, column_count, bond_width)
    )
    scale_factor = 1.0 / (physical * bond_width)
    whole_block = lax.all_gather(current_block, "state", axis=2, tiled=True)
    intersect = (
        lax.psum(jnp.sum(projected * whole_block.astype(jnp.float32)), "bond") * scale_factor
    )
    weight = penalty_weight[lax.axis_index("state")]
    summed = lax.psum_scatter(
        weight * intersect * projected, "state", scatter_dimension=2, tiled=True
    )
    penalized = current_block.astype(jnp.float32) + summed
    moved_all = lax.all_gather(moved, "state", axis=0, tiled=True)
    grown = jnp.einsum(
        "asf,ksea->kfe",
        lax.all_gather(current_site, "bond", axis=0, tiled=True),
        moved_all,
        preferred_element_type=jnp.float32,
    )
    intersect_next = lax.all_to_all(
        lax.all_to_all(
            grown.astype(jnp.bfloat16), "state", split_axis=0, concat_axis=1, tiled=True
        ),
        "bond",
        split_axis=1,
        concat_axis=2,
        tiled=True,
    )
    return (penalized, intersect_next)


def solution(mesh):
    placed = (
        P("state", "bond", None),
        P("state", None, "bond", None),
        P("state", None, "bond", None),
        P("bond", None, "state"),
        P(None, "bond", "state"),
        P(),
    )
    return jax.shard_map(
        shards,
        mesh=mesh,
        in_specs=placed,
        out_specs=(P(None, "bond", "state"), P("state", "bond", None)),
        check_vma=False,
    )
```

profile of v0, /device:TPU:0, one launch (start us, length us, event | category | flops | bytes accessed | tf_op | source)
XLA Modules:
  0.0 307.0 jit_solution(15348684443080593336)
XLA Ops:
  7.2 0.0 all-gather.5.cloned.1.call-start
  7.2 0.7 all-gather.5.cloned.1.call-update
  7.9 0.0 all-gather.7.cloned.1.call-start
  7.9 0.7 all-gather.7.cloned.1.call-update
  8.6 0.0 all-gather.11.cloned.1.call-start
  8.7 2.0 copy.15
  10.6 0.0 all-gather.11.cloned.1.call-update
  10.7 0.0 all-gather.9.cloned.1.call-start
  10.7 76.5 %all-gather.5.cloned.1.call-done = bf16[1,2048,2048]{2,1,0:T(8,128)(2,1)} async-done(((bf16[1,128,2048]{2,1,0:T(8,128)(2,1)}), bf16[1,2048,2048]{2,1,0:T(8,128)(2,1)}) %all-gather.5.cloned.1.call-update) | async-done | bytes 8388624 | tf_op jit(solution)/shard_map/all_gather | solution.py:25
  87.2 10.1 %fusion.2 = f32[768,2048]{1,0:T(8,128)S(1)} fusion(bf16[1,2048,2048]{2,1,0:T(8,128)(2,1)} %all-gather.5.cloned.1.call-done, bf16[256,2048]{1,0:T(8,128)(2,1)} %bitcast.45, bf16[512,2048]{1,0:T(8,128)(2,1)} %bitcast.44), kind=kOutput, calls=%fused_computation.2 | convolution fusion | flops 6448742400 | bytes 17825792 | tf_op jit(solution)/shard_map/dot_general | solution.py:8
  97.3 0.0 copy-start
  97.3 2.7 copy-done
  100.0 1.1 slice.13
  101.1 0.0 all-gather.9.cloned.1.call-update
  101.1 0.0 reduce-scatter.2.cloned.1.call-start
  101.2 4.7 %slice.9 = f32[512,2048]{1,0:T(8,128)} slice(f32[768,2048]{1,0:T(8,128)} %copy-done), slice={[0:512], [0:2048]} | slice | bytes 8388608 | tf_op jit(solution)/shard_map/slice | solution.py:26
  105.9 0.0 copy-start.2
  105.9 14.6 %all-gather.7.cloned.1.call-done = bf16[4,128,2048]{2,1,0:T(8,128)(2,1)} async-done(((bf16[4,128,1024]{2,1,0:T(8,128)(2,1)}), bf16[4,128,2048]{2,1,0:T(8,128)(2,1)}) %all-gather.7.cloned.1.call-update) | async-done | bytes 2097168 | tf_op jit(solution)/shard_map/all_gather | solution.py:33
  120.4 4.6 %multiply_reduce_fusion = f32[]{:T(128)} fusion(f32[4,128,2048]{2,1,0:T(8,128)} %bitcast.37, bf16[4,128,2048]{2,1,0:T(8,128)(2,1)} %all-gather.7.cloned.1.call-done), kind=kLoop, calls=%fused_computation.4 | loop fusion | flops 3145727 | bytes 6291460 | tf_op jit(solution)/shard_map/reduce_sum | solution.py:35
  125.0 0.0 copy-done.2
  125.0 0.6 dynamic_slice.3
  125.7 34.8 %psum.7 = f32[]{:T(128)} all-reduce(f32[]{:T(128)} %multiply_reduce_fusion), channel_id=1, replica_groups=mesh['state'=2,'bond'=16] {'bond'}, use_global_device_ids=true, to_apply=%region_1.0 | all-reduce | flops 1 | bytes 8 | tf_op jit(solution)/shard_map/psum | solution.py:35
  161.7 4.8 %broadcast_multiply_fusion = f32[4,128,2048]{2,1,0:T(8,128)} fusion(f32[]{:T(128)S(6)} %mul.17, f32[768,2048]{1,0:T(8,128)} %copy-done), kind=kLoop, calls=%fused_computation.9 | loop fusion | flops 1048576 | bytes 8388612 | tf_op jit(solution)/shard_map/mul | solution.py:39
  166.5 0.0 reduce-scatter.2.cloned.1.call-update
  166.5 31.4 %all-gather.11.cloned.1.call-done = bf16[2048,2,1024]{2,0,1:T(8,128)(2,1)} async-done(((bf16[128,2,1024]{2,0,1:T(8,128)(2,1)}), bf16[2048,2,1024]{2,0,1:T(8,128)(2,1)}) %all-gather.11.cloned.1.call-update) | async-done | bytes 8388624 | tf_op jit(solution)/shard_map/all_gather | solution.py:45
  197.9 33.7 %all-gather.9.cloned.1.call-done = bf16[2,2,128,2048]{3,2,1,0:T(8,128)(2,1)} async-done(((bf16[1,2,128,2048]{3,2,1,0:T(8,128)(2,1)}), bf16[2,2,128,2048]{3,2,1,0:T(8,128)(2,1)}) %all-gather.9.cloned.1.call-update) | async-done | bytes 2097168 | tf_op jit(solution)/shard_map/all_gather | solution.py:42
  231.5 6.3 %fusion.13 = bf16[2,1024,128]{1,2,0:T(8,128)(2,1)S(1)} fusion(bf16[2,2,128,2048]{3,2,1,0:T(8,128)(2,1)} %all-gather.9.cloned.1.call-done, bf16[2048,2,1024]{2,0,1:T(8,128)(2,1)} %all-gather.11.cloned.1.call-done), kind=kOutput, calls=%fused_computation.13 | convolution fusion | flops 2147745792 | bytes 11010048 | tf_op jit(solution)/shard_map/asf,ksea->kfe/dot_general | solution.py:43
  237.9 17.0 %all_to_all.30 = bf16[2,1024,128]{1,2,0:T(8,128)(2,1)S(1)} all-to-all(bf16[2,1024,128]{1,2,0:T(8,128)(2,1)S(1)} %fusion.13), channel_id=1, replica_groups=mesh['state'=2,'bond'=16] {'state'}, dimensions={0} | all-to-all | bytes 1048576 | tf_op jit(solution)/shard_map/all_to_all | solution.py:50
  254.8 0.3 copy.16
  255.1 8.1 %copy.23 = bf16[1,2048,128]{2,0,1:T(2,128)(2,1)S(1)} copy(bf16[1,2048,128]{2,1,0:T(8,128)(2,1)S(1)} %bitcast.41) | data formatting | bytes 1048576 | tf_op jit(solution)/shard_map/all_to_all | solution.py:50
  263.3 0.5 broadcast
  263.8 0.0 copy-start.1
  263.8 11.6 %reduce = bf16[2048,128]{1,0:T(8,128)(2,1)S(1)} reduce(bf16[2048,1,128]{2,1,0:T(2,128)(2,1)S(1)} %bitcast.40, bf16[]{:T(256)} %broadcast), dimensions={1}, to_apply=%bitcast.36.reduce_sub_computation | reduce | bytes 1048578
  275.4 0.1 reshape.17
  275.5 19.7 %all_to_all.31 = bf16[16,2,8192]{2,1,0:T(2,128)(2,1)S(1)} all-to-all(bf16[16,2,8192]{2,1,0:T(2,128)(2,1)S(1)} %reshape.17), channel_id=1, replica_groups=mesh['state'=2,'bond'=16] {'bond'}, dimensions={0} | all-to-all | bytes 1048576 | tf_op jit(solution)/shard_map/all_to_all | solution.py:49
  295.2 0.5 reshape.18
  295.7 0.1 copy.21
  295.8 0.3 copy.18
  296.1 1.0 copy.19
  297.1 0.0 reduce-scatter.2.cloned.1.call-done
  297.1 0.0 copy-done.1
  297.1 3.4 %convert_add_fusion = f32[4,128,1024]{2,1,0:T(8,128)} fusion(f32[4,128,1024]{2,1,0:T(8,128)} %reduce-scatter.2.cloned.1.call-done, bf16[4,128,1024]{2,1,0:T(8,128)(2,1)S(1)} %copy-done.1), kind=kLoop, calls=%fused_computation.10 | loop fusion | flops 1048576 | bytes 5242880 | tf_op jit(solution)/shard_map/add | solution.py:41
Async XLA Ops:
  7.2 80.0 %all-gather.5.cloned.1.call-start = ((), (), s32[]{:S(2)}) async-start(), calls=%async_computation.3 | async-start | bytes 8912896 | tf_op jit(solution)/shard_map/all_gather | solution.py:25
  7.9 112.5 %all-gather.7.cloned.1.call-start = ((), (), s32[]{:S(2)}) async-start(), calls=%async_computation.4 | async-start | bytes 3145728 | tf_op jit(solution)/shard_map/all_gather | solution.py:33
  8.6 189.2 %all-gather.11.cloned.1.call-start = ((), (), s32[]{:S(2)}) async-start(), calls=%async_computation.7 | async-start | bytes 8912896 | tf_op jit(solution)/shard_map/all_gather | solution.py:45
  10.7 220.9 %all-gather.9.cloned.1.call-start = ((), (), s32[]{:S(2)}) async-start(), calls=%async_computation.6 | async-start | bytes 3145728 | tf_op jit(solution)/shard_map/all_gather | solution.py:42
  97.3 2.7 copy-start
  101.1 196.0 %reduce-scatter.2.cloned.1.call-start = ((), (), s32[]{:S(2)}) async-start(), calls=%async_computation.5 | async-start | bytes 6291456 | tf_op jit(solution)/shard_map/reduce_scatter | solution.py:38
  105.9 19.2 %copy-start.2 = (f32[2]{0:T(128)S(1)}, f32[2]{0:T(128)}, u32[]{:S(2)}) copy-start(f32[2]{0:T(128)} %param.11) | copy-start | bytes 28
  263.8 33.3 %copy-start.1 = (bf16[4,128,1024]{2,1,0:T(8,128)(2,1)S(1)}, bf16[4,128,1024]{2,1,0:T(8,128)(2,1)}, u32[]{:S(2)}) copy-start(bf16[4,128,1024]{2,1,0:T(8,128)(2,1)} %param.10) | copy-start | bytes 3145732
Sparse Core Ops, SparseCore 0:
  10.1 77.0 all-gather.4
  88.7 31.6 all-gather.6
  123.2 74.6 all-gather.10
  199.8 31.6 all-gather.8
  233.7 59.9 reduce-scatter.1
where the time goes:
time: 307 us
  waiting for transfers between devices  158 us (51%)
  blocking collectives  71.4 us (23%)
  other arithmetic  24.3 us (8%)
  local copies, waits for them, and re-layouts  22 us (7%)
  matrix products  16.5 us (5%)
  between operations  15.1 us (5%)
    all_gather x1, waiting for transfers between devices, shards(): lax.all_gather(intersect_left, 'bond', axis=1, tiled=True)[0]  76.5 us
    psum x1, blocking collectives, shards(): lax.psum(jnp.sum(projected * whole_block.astype(jnp.float32)), 'bond')  34.8 us
    all_gather x1, waiting for transfers between devices, shards(): moved_all = lax.all_gather(moved, 'state', axis=0, tiled=True)  33.7 us
    all_gather x1, waiting for transfers between devices, shards(): lax.all_gather(current_site, 'bond', axis=0, tiled=True)  31.4 us
    all_to_all x1, blocking collectives, shards(): lax.all_to_all(lax.all_to_all(grown.astype(jnp.bfloat16), 'state', split_...  19.7 us
    all_to_all x1, blocking collectives, shards(): lax.all_to_all(grown.astype(jnp.bfloat16), 'state', split_axis=0, concat_...  17 us
    all_gather x1, waiting for transfers between devices, shards(): whole_block = lax.all_gather(current_block, 'state', axis=2, tiled=True)  14.6 us
    unnamed x1, other arithmetic  11.6 us
  transfers between devices with their start and end apart: 5, of which 4 were waited for; matrix products, arithmetic and copies ran while one was open for 18% of the time, Pallas kernels for 0%

commit v1 on v0

--- a/solution.py
+++ b/solution.py
@@ -40,12 +40,38 @@
     )
     penalized = current_block.astype(jnp.float32) + summed
     moved_all = lax.all_gather(moved, "state", axis=0, tiled=True)
-    grown = jnp.einsum(
+    devices, mine, extent = (lax.axis_size("bond"), lax.axis_index("bond"), current_site.shape[0])
+    upward = [(i, (i + 1) % devices) for i in range(devices)]
+    left_2 = [(i, (i - 1) % devices) for i in range(devices)]
+    halfway = devices // 2
+    from_left = from_right = current_site
+    so_far = jnp.einsum(
         "asf,ksea->kfe",
-        lax.all_gather(current_site, "bond", axis=0, tiled=True),
-        moved_all,
+        current_site,
+        lax.dynamic_slice_in_dim(moved_all, mine * extent, current_site.shape[0], axis=3),
         preferred_element_type=jnp.float32,
     )
+    for lap in range(1, halfway + 1):
+        from_left = lax.ppermute(from_left, "bond", upward)
+        if lap < devices - halfway:
+            from_right = lax.ppermute(from_right, "bond", left_2)
+            so_far = so_far + jnp.einsum(
+                "asf,ksea->kfe",
+                from_right,
+                lax.dynamic_slice_in_dim(
+                    moved_all, (mine + lap) % devices * extent, from_right.shape[0], axis=3
+                ),
+                preferred_element_type=jnp.float32,
+            )
+        so_far = so_far + jnp.einsum(
+            "asf,ksea->kfe",
+            from_left,
+            lax.dynamic_slice_in_dim(
+                moved_all, (mine - lap) % devices * extent, from_left.shape[0], axis=3
+            ),
+            preferred_element_type=jnp.float32,
+        )
+    grown = so_far
     intersect_next = lax.all_to_all(
         lax.all_to_all(
             grown.astype(jnp.bfloat16), "state", split_axis=0, concat_axis=1, tiled=True

time: 307 us -> 326 us (1.062)
  starting transfers between devices: 0.2 us -> 54.3 us
  waiting for transfers between devices: 158 us -> 123 us
  blocking collectives: 71.4 us -> 65.4 us
  matrix products: 16.5 us -> 20.6 us
    ppermute x0 -> x15, starting transfers between devices: none -> 54.1 us  [the longest x8 41.6 us: shards(): from_left = lax.ppermute(from_left, 'bond', upward)]
    all_gather x1, waiting for transfers between devices: 33.7 us -> 0.01 us  [shards(): moved_all = lax.all_gather(moved, 'state', axis=0, tiled=True)]
    all_gather x1 -> x0, waiting for transfers between devices: 31.4 us -> none  [shards(): lax.all_gather(current_site, 'bond', axis=0, tiled=True)]
    ppermute x0 -> x15, waiting for transfers between devices: none -> 28.6 us  [the longest x8 16.6 us: shards(): from_left = lax.ppermute(from_left, 'bond', upward)]
    all_to_all x1, blocking collectives: 17 us -> 10.3 us  [shards(): lax.all_to_all(grown.astype(jnp.bfloat16), 'state', split_axis=0, concat_...]
    dot_general x1 -> x16, matrix products: 6.34 us -> 10.5 us  [the longest x7 5.36 us: shards(): jnp.einsum('asf,ksea->kfe', from_right, lax.dynamic_slice_in_dim(moved_al...]
    unnamed x12 -> x40, local copies, waits for them, and re-layouts: 6.89 us -> 7.58 us
  transfers between devices with their start and end apart: 5 -> 19, of which waited for: 4 -> 10; matrix products, arithmetic and copies ran while one was open for 18% -> 18% of each run, Pallas kernels for 0% -> 0%
where the time goes in v1:
time: 326 us; the launch traced here: 325 us
  waiting for transfers between devices  123 us (38%)
  blocking collectives  65.4 us (20%)
  starting transfers between devices  54.3 us (17%)
  other arithmetic  24.3 us (7%)
  local copies, waits for them, and re-layouts  22.7 us (7%)
  matrix products  20.6 us (6%)
  between operations  15.4 us (5%)
    all_gather x1, waiting for transfers between devices, shards(): lax.all_gather(intersect_left, 'bond', axis=1, tiled=True)[0]  78.5 us
    ppermute x8, starting transfers between devices, shards(): from_left = lax.ppermute(from_left, 'bond', upward)  41.6 us
    psum x1, blocking collectives, shards(): lax.psum(jnp.sum(projected * whole_block.astype(jnp.float32)), 'bond')  33.7 us
    all_to_all x1, blocking collectives, shards(): lax.all_to_all(lax.all_to_all(grown.astype(jnp.bfloat16), 'state', split_...  21.4 us
    ppermute x8, waiting for transfers between devices, shards(): from_left = lax.ppermute(from_left, 'bond', upward)  16.6 us
    all_gather x1, waiting for transfers between devices, shards(): whole_block = lax.all_gather(current_block, 'state', axis=2, tiled=True)  14.1 us
    ppermute x7, starting transfers between devices, shards(): from_right = lax.ppermute(from_right, 'bond', left_2)  12.5 us
    ppermute x7, waiting for transfers between devices, shards(): from_right = lax.ppermute(from_right, 'bond', left_2)  12 us
  transfers between devices with their start and end apart: 19, of which 10 were waited for; matrix products, arithmetic and copies ran while one was open for 18% of the time, Pallas kernels for 0%

profile of v1, /device:TPU:0, one launch (start us, length us, event | category | flops | bytes accessed | tf_op | source)
XLA Modules:
  0.0 325.3 jit_solution(3569771426711832778)
XLA Ops:
  7.2 0.7 all-gather.4.cloned.1.call-update
  7.9 0.7 all-gather.6.cloned.1.call-update
  8.7 78.5 %all-gather.4.cloned.1.call-done = bf16[1,2048,2048]{2,1,0:T(8,128)(2,1)} async-done(((bf16[1,128,2048]{2,1,0:T(8,128)(2,1)}), bf16[1,2048,2048]{2,1,0:T(8,128)(2,1)}) %all-gather.4.cloned.1.call-update) | async-done | bytes 8388624 | tf_op jit(solution)/shard_map/all_gather | solution.py:25
  87.2 10.1 %fusion = f32[768,2048]{1,0:T(8,128)S(1)} fusion(bf16[1,2048,2048]{2,1,0:T(8,128)(2,1)} %all-gather.4.cloned.1.call-done, bf16[256,2048]{1,0:T(8,128)(2,1)} %bitcast.158, bf16[512,2048]{1,0:T(8,128)(2,1)} %bitcast.157), kind=kOutput, calls=%fused_computation | convolution fusion | flops 6448742400 | bytes 17825792 | tf_op jit(solution)/shard_map/dot_general | solution.py:8
  97.3 2.6 copy-done
  99.9 1.1 slice.13
  101.6 4.7 %slice.9 = f32[512,2048]{1,0:T(8,128)} slice(f32[768,2048]{1,0:T(8,128)} %copy-done), slice={[0:512], [0:2048]} | slice | bytes 8388608 | tf_op jit(solution)/shard_map/slice | solution.py:26
  106.3 14.1 %all-gather.6.cloned.1.call-done = bf16[4,128,2048]{2,1,0:T(8,128)(2,1)} async-done(((bf16[4,128,1024]{2,1,0:T(8,128)(2,1)}), bf16[4,128,2048]{2,1,0:T(8,128)(2,1)}) %all-gather.6.cloned.1.call-update) | async-done | bytes 2097168 | tf_op jit(solution)/shard_map/all_gather | solution.py:33
  120.4 4.6 %multiply_reduce_fusion = f32[]{:T(128)} fusion(f32[4,128,2048]{2,1,0:T(8,128)} %bitcast.150, bf16[4,128,2048]{2,1,0:T(8,128)(2,1)} %all-gather.6.cloned.1.call-done), kind=kLoop, calls=%fused_computation.2 | loop fusion | flops 3145727 | bytes 6291460 | tf_op jit(solution)/shard_map/reduce_sum | solution.py:35
  125.1 0.6 dynamic_slice.51
  125.7 33.7 %psum.7 = f32[]{:T(128)} all-reduce(f32[]{:T(128)} %multiply_reduce_fusion), channel_id=1, replica_groups=mesh['state'=2,'bond'=16] {'bond'}, use_global_device_ids=true, to_apply=%region_1.0 | all-reduce | flops 1 | bytes 8 | tf_op jit(solution)/shard_map/psum | solution.py:35
  160.7 4.8 %broadcast_multiply_fusion = f32[4,128,2048]{2,1,0:T(8,128)} fusion(f32[]{:T(128)S(6)} %mul.65, f32[768,2048]{1,0:T(8,128)} %copy-done), kind=kLoop, calls=%fused_computation.7 | loop fusion | flops 1048576 | bytes 8388612 | tf_op jit(solution)/shard_map/mul | solution.py:39
  165.6 0.5 collective-permute-start.3
  166.0 6.2 %collective-permute-done = bf16[128,2,1024]{2,0,1:T(8,128)(2,1)S(1)} collective-permute-done((bf16[128,2,1024]{2,0,1:T(8,128)(2,1)S(1)}, bf16[128,2,1024]{2,0,1:T(8,128)(2,1)S(1)}, u32[]{:S(2)}, u32[]{:S(2)}) %collective-permute-start) | collective-permute-done | bytes 524320 | tf_op jit(solution)/shard_map/ppermute | solution.py:57
  172.2 4.6 %collective-permute-start.2 = (bf16[128,2,1024]{2,0,1:T(8,128)(2,1)S(1)}, bf16[128,2,1024]{2,0,1:T(8,128)(2,1)S(1)}, u32[]{:S(2)}, u32[]{:S(2)}) collective-permute-start(bf16[128,2,1024]{2,0,1:T(8,128)(2,1)S(1)} %collective-permute-done), channel_id=1, source_target_pairs={{0,15},{1,0},{2,1},{3,2},{4,3},{5,4},{6,5},{7,6},{8,7},{9,8},{10,9... | collective-permute-start | bytes 1572872 | tf_op jit(solution)/shard_map/ppermute | solution.py:57
  177.0 0.8 collective-permute-start.5
  177.8 5.8 %collective-permute-done.2 = bf16[128,2,1024]{2,0,1:T(8,128)(2,1)S(1)} collective-permute-done((bf16[128,2,1024]{2,0,1:T(8,128)(2,1)S(1)}, bf16[128,2,1024]{2,0,1:T(8,128)(2,1)S(1)}, u32[]{:S(2)}, u32[]{:S(2)}) %collective-permute-start.2) | collective-permute-done | bytes 524320 | tf_op jit(solution)/shard_map/ppermute | solution.py:57
  183.5 4.7 %collective-permute-start.4 = (bf16[128,2,1024]{2,0,1:T(8,128)(2,1)S(1)}, bf16[128,2,1024]{2,0,1:T(8,128)(2,1)S(1)}, u32[]{:S(2)}, u32[]{:S(2)}) collective-permute-start(bf16[128,2,1024]{2,0,1:T(8,128)(2,1)S(1)} %collective-permute-done.2), channel_id=1, source_target_pairs={{0,15},{1,0},{2,1},{3,2},{4,3},{5,4},{6,5},{7,6},{8,7},{9,8},{10,9... | collective-permute-start | bytes 1572872 | tf_op jit(solution)/shard_map/ppermute | solution.py:57
  188.4 8.2 %collective-permute-start.7 = (bf16[128,2,1024]{2,0,1:T(8,128)(2,1)S(1)}, bf16[128,2,1024]{2,0,1:T(8,128)(2,1)S(1)}, u32[]{:S(2)}, u32[]{:S(2)}) collective-permute-start(bf16[128,2,1024]{2,0,1:T(8,128)(2,1)S(1)} %collective-permute-done.5), channel_id=1, source_target_pairs={{0,1},{1,2},{2,3},{3,4},{4,5},{5,6},{6,7},{7,8},{8,9},{9,10},{10,1... | collective-permute-start | bytes 1572872 | tf_op jit(solution)/shard_map/ppermute | solution.py:55
  196.6 3.0 collective-permute-start.6
  199.6 1.3 collective-permute-done.7
  201.0 9.9 %collective-permute-start.9 = (bf16[128,2,1024]{2,0,1:T(8,128)(2,1)S(1)}, bf16[128,2,1024]{2,0,1:T(8,128)(2,1)S(1)}, u32[]{:S(2)}, u32[]{:S(2)}) collective-permute-start(bf16[128,2,1024]{2,0,1:T(8,128)(2,1)S(1)} %collective-permute-done.7), channel_id=1, source_target_pairs={{0,1},{1,2},{2,3},{3,4},{4,5},{5,6},{6,7},{7,8},{8,9},{9,10},{10,1... | collective-permute-start | bytes 1572872 | tf_op jit(solution)/shard_map/ppermute | solution.py:55
  211.0 4.7 %collective-permute-done.9 = bf16[128,2,1024]{2,0,1:T(8,128)(2,1)S(1)} collective-permute-done((bf16[128,2,1024]{2,0,1:T(8,128)(2,1)S(1)}, bf16[128,2,1024]{2,0,1:T(8,128)(2,1)S(1)}, u32[]{:S(2)}, u32[]{:S(2)}) %collective-permute-start.9) | collective-permute-done | bytes 524320 | tf_op jit(solution)/shard_map/ppermute | solution.py:55
  215.7 9.4 %collective-permute-start.11 = (bf16[128,2,1024]{2,0,1:T(8,128)(2,1)S(1)}, bf16[128,2,1024]{2,0,1:T(8,128)(2,1)S(1)}, u32[]{:S(2)}, u32[]{:S(2)}) collective-permute-start(bf16[128,2,1024]{2,0,1:T(8,128)(2,1)S(1)} %collective-permute-done.9), channel_id=1, source_target_pairs={{0,1},{1,2},{2,3},{3,4},{4,5},{5,6},{6,7},{7,8},{8,9},{9,10},{10,1... | collective-permute-start | bytes 1572872 | tf_op jit(solution)/shard_map/ppermute | solution.py:55
  225.1 5.2 %collective-permute-done.11 = bf16[128,2,1024]{2,0,1:T(8,128)(2,1)S(1)} collective-permute-done((bf16[128,2,1024]{2,0,1:T(8,128)(2,1)S(1)}, bf16[128,2,1024]{2,0,1:T(8,128)(2,1)S(1)}, u32[]{:S(2)}, u32[]{:S(2)}) %collective-permute-start.11) | collective-permute-done | bytes 524320 | tf_op jit(solution)/shard_map/ppermute | solution.py:55
  230.3 9.1 %collective-permute-start.13 = (bf16[128,2,1024]{2,0,1:T(8,128)(2,1)S(1)}, bf16[128,2,1024]{2,0,1:T(8,128)(2,1)S(1)}, u32[]{:S(2)}, u32[]{:S(2)}) collective-permute-start(bf16[128,2,1024]{2,0,1:T(8,128)(2,1)S(1)} %collective-permute-done.11), channel_id=1, source_target_pairs={{0,1},{1,2},{2,3},{3,4},{4,5},{5,6},{6,7},{7,8},{8,9},{9,10},{10,1... | collective-permute-start | bytes 1572872 | tf_op jit(solution)/shard_map/ppermute | solution.py:55
  239.5 5.1 %collective-permute-done.13 = bf16[128,2,1024]{2,0,1:T(8,128)(2,1)S(1)} collective-permute-done((bf16[128,2,1024]{2,0,1:T(8,128)(2,1)S(1)}, bf16[128,2,1024]{2,0,1:T(8,128)(2,1)S(1)}, u32[]{:S(2)}, u32[]{:S(2)}) %collective-permute-start.13) | collective-permute-done | bytes 524320 | tf_op jit(solution)/shard_map/ppermute | solution.py:55
  244.6 3.4 %collective-permute-start.14 = (bf16[128,2,1024]{2,0,1:T(8,128)(2,1)S(1)}, bf16[128,2,1024]{2,0,1:T(8,128)(2,1)S(1)}, u32[]{:S(2)}, u32[]{:S(2)}) collective-permute-start(bf16[128,2,1024]{2,0,1:T(8,128)(2,1)S(1)} %collective-permute-done.13), channel_id=1, source_target_pairs={{0,1},{1,2},{2,3},{3,4},{4,5},{5,6},{6,7},{7,8},{8,9},{9,10},{10,1... | collective-permute-start | bytes 1572872 | tf_op jit(solution)/shard_map/ppermute | solution.py:55
  248.0 1.6 convolution_bitcast_fusion.5
  249.6 1.4 convolution_bitcast_fusion.7
  251.6 0.3 convolution_bitcast_fusion.13
  252.0 0.3 convolution_bitcast_fusion.15
  252.3 0.4 copy-done.9
  253.0 0.7 copy-done.11
  254.0 0.7 copy-done.13
  255.1 0.7 copy-done.15
  255.8 0.3 fusion.12
  256.1 1.4 fusion.14
  257.9 1.4 fusion.16
  259.6 1.4 fusion.18
  261.2 10.3 %all_to_all.30 = bf16[2,1024,128]{1,2,0:T(8,128)(2,1)S(1)} all-to-all(bf16[2,1024,128]{1,2,0:T(8,128)(2,1)S(1)} %fusion.21), channel_id=1, replica_groups=mesh['state'=2,'bond'=16] {'state'}, dimensions={0} | all-to-all | bytes 1048576 | tf_op jit(solution)/shard_map/all_to_all | solution.py:76
  271.8 8.1 %copy.50 = bf16[1,2048,128]{2,0,1:T(2,128)(2,1)S(1)} copy(bf16[1,2048,128]{2,1,0:T(8,128)(2,1)S(1)} %bitcast.154) | data formatting | bytes 1048576 | tf_op jit(solution)/shard_map/all_to_all | solution.py:76
  279.9 0.5 broadcast.15
  280.5 11.5 %reduce = bf16[2048,128]{1,0:T(8,128)(2,1)S(1)} reduce(bf16[2048,1,128]{2,1,0:T(2,128)(2,1)S(1)} %bitcast.153, bf16[]{:T(256)} %broadcast.15), dimensions={1}, to_apply=%bitcast.149.reduce_sub_computation | reduce | bytes 1048578
  292.1 21.4 %all_to_all.31 = bf16[16,2,8192]{2,1,0:T(2,128)(2,1)S(1)} all-to-all(bf16[16,2,8192]{2,1,0:T(2,128)(2,1)S(1)} %reshape.47), channel_id=1, replica_groups=mesh['state'=2,'bond'=16] {'bond'}, dimensions={0} | all-to-all | bytes 1048576 | tf_op jit(solution)/shard_map/all_to_all | solution.py:75
  313.5 0.5 reshape.48
  314.4 1.0 copy.27
  315.5 3.4 %convert_add_fusion = f32[4,128,1024]{2,1,0:T(8,128)} fusion(f32[4,128,1024]{2,1,0:T(8,128)} %reduce-scatter.2.cloned.1.call-done, bf16[4,128,1024]{2,1,0:T(8,128)(2,1)S(1)} %copy-done.1), kind=kLoop, calls=%fused_computation.8 | loop fusion | flops 1048576 | bytes 5242880 | tf_op jit(solution)/shard_map/add | solution.py:41
  (64 shorter events, 4.4 us)
Async XLA Ops:
  7.2 80.0 %all-gather.4.cloned.1.call-start = ((), (), s32[]{:S(2)}) async-start(), calls=%async_computation.3 | async-start | bytes 8912896 | tf_op jit(solution)/shard_map/all_gather | solution.py:25
  7.9 112.5 %all-gather.6.cloned.1.call-start = ((), (), s32[]{:S(2)}) async-start(), calls=%async_computation.4 | async-start | bytes 3145728 | tf_op jit(solution)/shard_map/all_gather | solution.py:33
  8.6 239.4 %all-gather.8.cloned.1.call-start = ((), (), s32[]{:S(2)}) async-start(), calls=%async_computation.6 | async-start | bytes 3145728 | tf_op jit(solution)/shard_map/all_gather | solution.py:42
  97.3 2.6 copy-start
  99.9 1.2 copy-start.3
  101.1 214.4 %reduce-scatter.2.cloned.1.call-start = ((), (), s32[]{:S(2)}) async-start(), calls=%async_computation.5 | async-start | bytes 6291456 | tf_op jit(solution)/shard_map/reduce_scatter | solution.py:38
  101.2 64.3 %collective-permute-start.1 = (bf16[128,2,1024]{2,0,1:T(8,128)(2,1)S(1)}, bf16[128,2,1024]{2,0,1:T(8,128)(2,1)S(1)}, u32[]{:S(2)}, u32[]{:S(2)}) collective-permute-start(bf16[128,2,1024]{2,0,1:T(8,128)(2,1)S(1)} %copy.21), channel_id=1, source_target_pairs={{0,1},{1,2},{2,3},{3,4},{4,5},{5,6},{6,7},{7,8},{8,9},{9,10},{10,1... | collective-permute-start | bytes 1572872 | tf_op jit(solution)/shard_map/ppermute | solution.py:55
  120.4 4.6 %copy-start.16 = (f32[2]{0:T(128)S(1)}, f32[2]{0:T(128)}, u32[]{:S(2)}) copy-start(f32[2]{0:T(128)} %param.11) | copy-start | bytes 28
  165.5 6.8 %collective-permute-start = (bf16[128,2,1024]{2,0,1:T(8,128)(2,1)S(1)}, bf16[128,2,1024]{2,0,1:T(8,128)(2,1)S(1)}, u32[]{:S(2)}, u32[]{:S(2)}) collective-permute-start(bf16[128,2,1024]{2,0,1:T(8,128)(2,1)S(1)} %copy.21), channel_id=1, source_target_pairs={{0,15},{1,0},{2,1},{3,2},{4,3},{5,4},{6,5},{7,6},{8,7},{9,8},{10,9... | collective-permute-start | bytes 1572872 | tf_op jit(solution)/shard_map/ppermute | solution.py:57
  165.6 11.5 %collective-permute-start.3 = (bf16[128,2,1024]{2,0,1:T(8,128)(2,1)S(1)}, bf16[128,2,1024]{2,0,1:T(8,128)(2,1)S(1)}, u32[]{:S(2)}, u32[]{:S(2)}) collective-permute-start(bf16[128,2,1024]{2,0,1:T(8,128)(2,1)S(1)} %collective-permute-done.1), channel_id=1, source_target_pairs={{0,1},{1,2},{2,3},{3,4},{4,5},{5,6},{6,7},{7,8},{8,9},{9,10},{10,1... | collective-permute-start | bytes 1572872 | tf_op jit(solution)/shard_map/ppermute | solution.py:55
  172.2 27.4 %copy-start.8 = (bf16[128,2,1024]{2,0,1:T(8,128)(2,1)}, bf16[128,2,1024]{2,0,1:T(8,128)(2,1)S(1)}, u32[]{:S(2)}) copy-start(bf16[128,2,1024]{2,0,1:T(8,128)(2,1)S(1)} %collective-permute-done) | copy-start | bytes 1572868
  172.2 11.3 %collective-permute-start.2 = (bf16[128,2,1024]{2,0,1:T(8,128)(2,1)S(1)}, bf16[128,2,1024]{2,0,1:T(8,128)(2,1)S(1)}, u32[]{:S(2)}, u32[]{:S(2)}) collective-permute-start(bf16[128,2,1024]{2,0,1:T(8,128)(2,1)S(1)} %collective-permute-done), channel_id=1, source_target_pairs={{0,15},{1,0},{2,1},{3,2},{4,3},{5,4},{6,5},{7,6},{8,7},{9,8},{10,9... | collective-permute-start | bytes 1572872 | tf_op jit(solution)/shard_map/ppermute | solution.py:57
  177.0 11.4 %collective-permute-start.5 = (bf16[128,2,1024]{2,0,1:T(8,128)(2,1)S(1)}, bf16[128,2,1024]{2,0,1:T(8,128)(2,1)S(1)}, u32[]{:S(2)}, u32[]{:S(2)}) collective-permute-start(bf16[128,2,1024]{2,0,1:T(8,128)(2,1)S(1)} %collective-permute-done.3), channel_id=1, source_target_pairs={{0,1},{1,2},{2,3},{3,4},{4,5},{5,6},{6,7},{7,8},{8,9},{9,10},{10,1... | collective-permute-start | bytes 1572872 | tf_op jit(solution)/shard_map/ppermute | solution.py:55
  183.5 46.7 %copy-start.10 = (bf16[128,2,1024]{2,0,1:T(8,128)(2,1)}, bf16[128,2,1024]{2,0,1:T(8,128)(2,1)S(1)}, u32[]{:S(2)}) copy-start(bf16[128,2,1024]{2,0,1:T(8,128)(2,1)S(1)} %collective-permute-done.2) | copy-start | bytes 1572868
  183.5 13.1 %collective-permute-start.4 = (bf16[128,2,1024]{2,0,1:T(8,128)(2,1)S(1)}, bf16[128,2,1024]{2,0,1:T(8,128)(2,1)S(1)}, u32[]{:S(2)}, u32[]{:S(2)}) collective-permute-start(bf16[128,2,1024]{2,0,1:T(8,128)(2,1)S(1)} %collective-permute-done.2), channel_id=1, source_target_pairs={{0,15},{1,0},{2,1},{3,2},{4,3},{5,4},{6,5},{7,6},{8,7},{9,8},{10,9... | collective-permute-start | bytes 1572872 | tf_op jit(solution)/shard_map/ppermute | solution.py:57
  188.4 12.6 %collective-permute-start.7 = (bf16[128,2,1024]{2,0,1:T(8,128)(2,1)S(1)}, bf16[128,2,1024]{2,0,1:T(8,128)(2,1)S(1)}, u32[]{:S(2)}, u32[]{:S(2)}) collective-permute-start(bf16[128,2,1024]{2,0,1:T(8,128)(2,1)S(1)} %collective-permute-done.5), channel_id=1, source_target_pairs={{0,1},{1,2},{2,3},{3,4},{4,5},{5,6},{6,7},{7,8},{8,9},{9,10},{10,1... | collective-permute-start | bytes 1572872 | tf_op jit(solution)/shard_map/ppermute | solution.py:55
  196.6 33.7 %copy-start.12 = (bf16[128,2,1024]{2,0,1:T(8,128)(2,1)}, bf16[128,2,1024]{2,0,1:T(8,128)(2,1)S(1)}, u32[]{:S(2)}) copy-start(bf16[128,2,1024]{2,0,1:T(8,128)(2,1)S(1)} %collective-permute-done.4) | copy-start | bytes 1572868
  196.6 14.2 %collective-permute-start.6 = (bf16[128,2,1024]{2,0,1:T(8,128)(2,1)S(1)}, bf16[128,2,1024]{2,0,1:T(8,128)(2,1)S(1)}, u32[]{:S(2)}, u32[]{:S(2)}) collective-permute-start(bf16[128,2,1024]{2,0,1:T(8,128)(2,1)S(1)} %collective-permute-done.4), channel_id=1, source_target_pairs={{0,15},{1,0},{2,1},{3,2},{4,3},{5,4},{6,5},{7,6},{8,7},{9,8},{10,9... | collective-permute-start | bytes 1572872 | tf_op jit(solution)/shard_map/ppermute | solution.py:57
  201.0 10.0 %copy-start.6 = (bf16[128,2,1024]{2,0,1:T(8,128)(2,1)}, bf16[128,2,1024]{2,0,1:T(8,128)(2,1)S(1)}, u32[]{:S(2)}) copy-start(bf16[128,2,1024]{2,0,1:T(8,128)(2,1)S(1)} %collective-permute-done.7) | copy-start | bytes 1572868
  201.0 14.7 %collective-permute-start.9 = (bf16[128,2,1024]{2,0,1:T(8,128)(2,1)S(1)}, bf16[128,2,1024]{2,0,1:T(8,128)(2,1)S(1)}, u32[]{:S(2)}, u32[]{:S(2)}) collective-permute-start(bf16[128,2,1024]{2,0,1:T(8,128)(2,1)S(1)} %collective-permute-done.7), channel_id=1, source_target_pairs={{0,1},{1,2},{2,3},{3,4},{4,5},{5,6},{6,7},{7,8},{8,9},{9,10},{10,1... | collective-permute-start | bytes 1572872 | tf_op jit(solution)/shard_map/ppermute | solution.py:55
  210.9 19.4 %copy-start.14 = (bf16[128,2,1024]{2,0,1:T(8,128)(2,1)}, bf16[128,2,1024]{2,0,1:T(8,128)(2,1)S(1)}, u32[]{:S(2)}) copy-start(bf16[128,2,1024]{2,0,1:T(8,128)(2,1)S(1)} %collective-permute-done.6) | copy-start | bytes 1572868
  210.9 14.2 %collective-permute-start.8 = (bf16[128,2,1024]{2,0,1:T(8,128)(2,1)S(1)}, bf16[128,2,1024]{2,0,1:T(8,128)(2,1)}, u32[]{:S(2)}, u32[]{:S(2)}) collective-permute-start(bf16[128,2,1024]{2,0,1:T(8,128)(2,1)S(1)} %collective-permute-done.6), channel_id=1, source_target_pairs={{0,15},{1,0},{2,1},{3,2},{4,3},{5,4},{6,5},{7,6},{8,7},{9,8},{10,9... | collective-permute-start | bytes 1572872 | tf_op jit(solution)/shard_map/ppermute | solution.py:57
  215.7 14.6 %copy-start.7 = (bf16[128,2,1024]{2,0,1:T(8,128)(2,1)}, bf16[128,2,1024]{2,0,1:T(8,128)(2,1)S(1)}, u32[]{:S(2)}) copy-start(bf16[128,2,1024]{2,0,1:T(8,128)(2,1)S(1)} %collective-permute-done.9) | copy-start | bytes 1572868
  215.7 14.6 %collective-permute-start.11 = (bf16[128,2,1024]{2,0,1:T(8,128)(2,1)S(1)}, bf16[128,2,1024]{2,0,1:T(8,128)(2,1)S(1)}, u32[]{:S(2)}, u32[]{:S(2)}) collective-permute-start(bf16[128,2,1024]{2,0,1:T(8,128)(2,1)S(1)} %collective-permute-done.9), channel_id=1, source_target_pairs={{0,1},{1,2},{2,3},{3,4},{4,5},{5,6},{6,7},{7,8},{8,9},{9,10},{10,1... | collective-permute-start | bytes 1572872 | tf_op jit(solution)/shard_map/ppermute | solution.py:55
  225.1 14.3 %collective-permute-start.10 = (bf16[128,2,1024]{2,0,1:T(8,128)(2,1)}, bf16[128,2,1024]{2,0,1:T(8,128)(2,1)}, u32[]{:S(2)}, u32[]{:S(2)}) collective-permute-start(bf16[128,2,1024]{2,0,1:T(8,128)(2,1)} %collective-permute-done.8), channel_id=1, source_target_pairs={{0,15},{1,0},{2,1},{3,2},{4,3},{5,4},{6,5},{7,6},{8,7},{9,8},{10,9... | collective-permute-start | bytes 1572872 | tf_op jit(solution)/shard_map/ppermute | solution.py:57
  230.3 9.2 %copy-start.4 = (bf16[128,2,1024]{2,0,1:T(8,128)(2,1)}, bf16[128,2,1024]{2,0,1:T(8,128)(2,1)S(1)}, u32[]{:S(2)}) copy-start(bf16[128,2,1024]{2,0,1:T(8,128)(2,1)S(1)} %collective-permute-done.11) | copy-start | bytes 1572868
  230.3 14.2 %collective-permute-start.13 = (bf16[128,2,1024]{2,0,1:T(8,128)(2,1)S(1)}, bf16[128,2,1024]{2,0,1:T(8,128)(2,1)S(1)}, u32[]{:S(2)}, u32[]{:S(2)}) collective-permute-start(bf16[128,2,1024]{2,0,1:T(8,128)(2,1)S(1)} %collective-permute-done.11), channel_id=1, source_target_pairs={{0,1},{1,2},{2,3},{3,4},{4,5},{5,6},{6,7},{7,8},{8,9},{9,10},{10,1... | collective-permute-start | bytes 1572872 | tf_op jit(solution)/shard_map/ppermute | solution.py:55
  239.4 20.2 %collective-permute-start.12 = (bf16[128,2,1024]{2,0,1:T(8,128)(2,1)}, bf16[128,2,1024]{2,0,1:T(8,128)(2,1)}, u32[]{:S(2)}, u32[]{:S(2)}) collective-permute-start(bf16[128,2,1024]{2,0,1:T(8,128)(2,1)} %collective-permute-done.10), channel_id=1, source_target_pairs={{0,15},{1,0},{2,1},{3,2},{4,3},{5,4},{6,5},{7,6},{8,7},{9,8},{10,9... | collective-permute-start | bytes 1572872 | tf_op jit(solution)/shard_map/ppermute | solution.py:57
  244.6 16.4 %collective-permute-start.14 = (bf16[128,2,1024]{2,0,1:T(8,128)(2,1)S(1)}, bf16[128,2,1024]{2,0,1:T(8,128)(2,1)S(1)}, u32[]{:S(2)}, u32[]{:S(2)}) collective-permute-start(bf16[128,2,1024]{2,0,1:T(8,128)(2,1)S(1)} %collective-permute-done.13), channel_id=1, source_target_pairs={{0,1},{1,2},{2,3},{3,4},{4,5},{5,6},{6,7},{7,8},{8,9},{9,10},{10,1... | collective-permute-start | bytes 1572872 | tf_op jit(solution)/shard_map/ppermute | solution.py:55
  248.0 3.0 copy-start.2
  251.6 1.0 copy-start.9
  252.7 1.0 copy-start.11
  253.7 1.0 copy-start.13
  254.8 1.0 copy-start.15
  256.1 1.4 copy-start.5
  314.1 1.4 copy-start.1
Sparse Core Ops, SparseCore 0:
  10.1 77.0 all-gather.3
  88.7 31.6 all-gather.5
  122.6 33.0 all-gather.7
  165.6 50.6 reduce-scatter.1
